TPU v7x, 256 devices: a whole 4x4x8 slice. The times are simulated.
256 devices in a mesh: dp: 16 (over z, core), feat: 16 (over x, y).
Axes of the slice: x: 4, y: 4, z: 8, core: 2. Of those that a mesh axis runs over, the one named last changes fastest.
Arguments:
- points: bfloat16 [4096, 256], P('dp'), may hold values from -6 to 6
- freqs: bfloat16 [256, 8192], P(None, 'feat'), may hold values from -0.375 to 0.375
- phase: float32 [8192], P('feat'), may hold values from -3.140625 to 3.140625
- ridge: float32 [8192], P('feat'), may hold values from 0.05 to 0.5
- targets: bfloat16 [8, 4096], P(None, 'dp'), may hold values from -6 to 6
Outputs:
- gram: float32 [8192, 8192], P('feat', 'dp')
- projected: float32 [8, 8192], P(None, 'feat')
- factors: float32 [8192, 1024], P('feat')
All inputs are finite; a program needn't handle non-finite values.
Results may differ from a plain program's by a relative error of at most 0.003.
Values may be sent and summed in bfloat16 or wider, within the bound.
A program may use at most 128 MiB of HBM per device.

v0:
```python
import math

import jax
import jax.numpy as jnp
from jax import lax
from jax.sharding import PartitionSpec as P

FB = 1024


def features(rows, freq_cols, phase_cols, scale):
    angle = jnp.dot(rows, freq_cols, preferred_element_type=jnp.float32) + phase_cols
    return (scale * jnp.cos(angle)).astype(jnp.bfloat16)


def cross(left, right):
    return lax.dot_general(
        left, right, (((0,), (0,)), ((), ())), preferred_element_type=jnp.float32
    )


def with_ridge(tile, ridge, row_start, col_start):
    rows_here = row_start + lax.broadcasted_iota(jnp.int32, tile.shape, 0)
    cols_here = col_start + lax.broadcasted_iota(jnp.int32, tile.shape, 1)
    return tile + jnp.where(rows_here == cols_here, ridge[:, None], 0.0)


def shards(points, freqs, phase, ridge, targets):
    data_count = lax.axis_size("dp")
    feat_count = lax.axis_size("feat")
    feat_index = lax.axis_index("feat")
    data_index = lax.axis_index("dp")
    local_width = freqs.shape[1]
    total_width = local_width * feat_count
    tile_width = total_width // data_count
    window = max(local_width, FB)
    window_start = feat_index * local_width // window * window
    row_start = feat_index * local_width
    col_start = data_index * tile_width
    scale = math.sqrt(2.0 / (points.shape[0] * data_count))
    points_all, targets_all = (
        lax.all_gather(points, "dp", axis=0, tiled=True),
        lax.all_gather(targets, "dp", axis=1, tiled=True),
    )
    freqs_wide, phase_all, ridge_all = (
        lax.all_gather(freqs.astype(jnp.float32), "feat", axis=1, tiled=True),
        lax.all_gather(phase, "feat", axis=0, tiled=True),
        lax.all_gather(ridge, "feat", axis=0, tiled=True),
    )
    freqs_all = freqs_wide.astype(jnp.bfloat16)
    row_phi = features(points_all, freqs, phase, scale)
    col_phi = features(
        points_all,
        lax.dynamic_slice_in_dim(freqs_all, col_start, tile_width, 1),
        lax.dynamic_slice_in_dim(phase_all, col_start, tile_width, 0),
        scale,
    )
    gram_tile = cross(row_phi, col_phi)
    window_phi = features(
        points_all,
        lax.dynamic_slice_in_dim(freqs_all, window_start, window, 1),
        lax.dynamic_slice_in_dim(phase_all, window_start, window, 0),
        scale,
    )
    projected = jnp.dot(targets_all, row_phi, preferred_element_type=jnp.float32)
    slab = cross(window_phi, window_phi)
    window_ridge = lax.dynamic_slice_in_dim(ridge_all, window_start, window, 0)
    slab = with_ridge(slab, window_ridge, window_start, window_start)
    gram_tile = with_ridge(gram_tile, ridge, row_start, col_start)
    block_count = window // FB
    stacked = jnp.stack([slab])
    factors_all = jnp.linalg.cholesky(stacked).reshape(window, FB)
    factor_rows = lax.dynamic_slice_in_dim(factors_all, row_start - window_start, local_width, 0)
    return (gram_tile, projected, factor_rows)


def solution(mesh):
    in_specs = (P("dp", None), P(None, "feat"), P("feat"), P("feat"), P(None, "dp"))
    out_specs = (P("feat", "dp"), P(None, "feat"), P("feat", None))
    return jax.shard_map(shards, mesh=mesh, in_specs=in_specs, out_specs=out_specs, check_vma=False)
```

profile of v0, /device:TPU:1, one launch (start us, length us, event | category | flops | bytes accessed | tf_op | source)
XLA Modules:
  0.0 462.6 jit_solution(10146078261034066194)
XLA Ops:
  7.2 0.7 all-gather.5.cloned.1.call-update
  7.9 0.7 all-gather.7.cloned.1.call-update
  8.7 19.1 %all-gather = f32[16,1,512]{2,1,0:T(1,128)S(1)} all-gather(f32[1,1,512]{2,1,0:T(1,128)} %bitcast.188), channel_id=1, replica_groups=mesh['dp'=16,'feat'=16] {'feat'}, dimensions={0}, use_global_device_ids=true | all-gather | bytes 34816 | tf_op jit(solution)/shard_map/all_gather | solution.py:47
  27.8 0.1 dynamic_slice.21
  27.9 18.0 %all-gather.1 = f32[16,1,512]{2,1,0:T(1,128)S(1)} all-gather(f32[1,1,512]{2,1,0:T(1,128)} %bitcast.189), channel_id=1, replica_groups=mesh['dp'=16,'feat'=16] {'feat'}, dimensions={0}, use_global_device_ids=true | all-gather | bytes 34816 | tf_op jit(solution)/shard_map/all_gather | solution.py:48
  45.9 30.9 %all_gather.18 = bf16[8,4096]{1,0:T(8,128)(2,1)S(1)} all-gather(bf16[8,256]{1,0:T(8,128)(2,1)} %param.9), channel_id=1, replica_groups=mesh['dp'=16,'feat'=16] {'dp'}, dimensions={1}, use_global_device_ids=true | all-gather | bytes 69632 | tf_op jit(solution)/shard_map/all_gather | solution.py:43
  76.9 29.4 %multiply_convert_fusion.2 = bf16[4096,512]{1,0:T(8,128)(2,1)S(1)} fusion(bf16[4096,256]{1,0:T(8,128)(2,1)} %all-gather.5.cloned.1.call-done, bf16[256,512]{1,0:T(8,128)(2,1)} %param.6, f32[512]{0:T(512)} %param.7), kind=kOutput, calls=%fused_computation.2 | convolution fusion | flops 1080033280 | bytes 6555648 | tf_op jit(solution)/shard_map/dot_general | solution.py:12
  106.3 1.9 copy-done.3
  108.3 1.3 convolution_bitcast_fusion.13
  109.5 4.9 %all-gather.7.cloned.1.call-done = bf16[256,8192]{1,0:T(8,128)(2,1)} async-done(((bf16[256,512]{1,0:T(8,128)(2,1)}), bf16[256,8192]{1,0:T(8,128)(2,1)}) %all-gather.7.cloned.1.call-update) | async-done | bytes 4194320 | tf_op jit(solution)/shard_map/all_gather | solution.py:46
  114.5 59.9 %multiply_convert_fusion.clone.6 = bf16[1024,4096]{1,0:T(8,128)(2,1)} fusion(bf16[4096,256]{1,0:T(8,128)(2,1)S(1)} %copy-done.6, f32[1024]{0:T(1024)S(1)} %dynamic_slice.23, bf16[256,8192]{1,0:T(8,128)(2,1)} %all-gather.7.cloned.1.call-done, s32[]{:T(128)S(6)} %select_n.32), kind=kOutput, calls=%fused_computation.clone.clone.clone.2 | convolution fusion | flops 2160066560 | bytes 11014148 | tf_op jit(solution)/shard_map/dot_general | solution.py:12
  174.3 26.7 %fusion = f32[1024,1024]{0,1:T(8,128)S(1)} fusion(bf16[1024,4096]{1,0:T(8,128)(2,1)} %multiply_convert_fusion.clone.6), kind=kOutput, calls=%fused_computation.3 | convolution fusion | flops 8589934592 | bytes 12582912 | tf_op jit(solution)/shard_map/dot_general | solution.py:17
  201.0 1.9 copy-done.1
  202.9 2.4 fusion.2
  205.4 5.3 %copy.11 = f32[1,1024,1024]{2,1,0:T(8,128)} copy(f32[1,1024,1024]{1,2,0:T(8,128)} %fusion.2) | data formatting | bytes 8388608 | tf_op jit(solution)/shard_map/stack | solution.py:71
  210.7 4.2 fusion.1
  214.9 1.9 copy-done.2
  216.9 11.7 %custom-call.67 = f32[1,128,128]{2,1,0:T(8,128)S(1)} custom-call(f32[1,128,128]{2,1,0:T(8,128)S(1)} %cholesky.585), custom_call_target="Cholesky" | custom-call | tf_op jit(solution)/shard_map/jit(cholesky)/cholesky | solution.py:72
  228.6 2.5 cholesky.249
  231.1 9.8 %custom-call.68 = f32[1,1,128,128]{2,3,1,0:T(8,128)S(1)} custom-call(f32[1,1,128,128]{3,2,1,0:T(8,128)S(1)} %get-tuple-element.24), custom_call_target="InvertDiagBlocksLowerTriangular" | custom-call | tf_op jit(solution)/shard_map/jit(cholesky)/cholesky | solution.py:72
  240.9 2.4 constant_dynamic-update-slice_fusion.7
  243.3 1.5 fusion.5
  244.9 11.7 %custom-call.69 = f32[1,128,128]{2,1,0:T(8,128)S(1)} custom-call(f32[1,128,128]{2,1,0:T(8,128)S(1)} %cholesky.589), custom_call_target="Cholesky" | custom-call | tf_op jit(solution)/shard_map/jit(cholesky)/cholesky | solution.py:72
  256.6 0.6 select_reduce_fusion.6
  257.2 10.2 %custom-call.70 = f32[1,1,128,128]{2,3,1,0:T(8,128)S(1)} custom-call(f32[1,1,128,128]{3,2,1,0:T(8,128)S(1)} %get-tuple-element.21), custom_call_target="InvertDiagBlocksLowerTriangular" | custom-call | tf_op jit(solution)/shard_map/jit(cholesky)/cholesky | solution.py:72
  267.4 1.2 fusion.6
  268.7 2.1 fusion.8
  270.8 11.7 %custom-call.71 = f32[1,128,128]{2,1,0:T(8,128)S(1)} custom-call(f32[1,128,128]{2,1,0:T(8,128)S(1)} %cholesky.594), custom_call_target="Cholesky" | custom-call | tf_op jit(solution)/shard_map/jit(cholesky)/cholesky | solution.py:72
  282.5 0.6 select_reduce_fusion.5
  283.1 9.8 %custom-call.72 = f32[1,1,128,128]{2,3,1,0:T(8,128)S(1)} custom-call(f32[1,1,128,128]{3,2,1,0:T(8,128)S(1)} %get-tuple-element.18), custom_call_target="InvertDiagBlocksLowerTriangular" | custom-call | tf_op jit(solution)/shard_map/jit(cholesky)/cholesky | solution.py:72
  292.9 1.2 fusion.7
  294.1 2.3 fusion.10
  296.4 11.9 %custom-call.73 = f32[1,128,128]{2,1,0:T(8,128)S(1)} custom-call(f32[1,128,128]{2,1,0:T(8,128)S(1)} %cholesky.599), custom_call_target="Cholesky" | custom-call | tf_op jit(solution)/shard_map/jit(cholesky)/cholesky | solution.py:72
  308.3 0.6 select_reduce_fusion.4
  309.0 9.8 %custom-call.74 = f32[1,1,128,128]{2,3,1,0:T(8,128)S(1)} custom-call(f32[1,1,128,128]{3,2,1,0:T(8,128)S(1)} %get-tuple-element.15), custom_call_target="InvertDiagBlocksLowerTriangular" | custom-call | tf_op jit(solution)/shard_map/jit(cholesky)/cholesky | solution.py:72
  318.8 1.1 fusion.9
  319.9 2.3 fusion.11
  322.2 11.7 %custom-call.75 = f32[1,128,128]{2,1,0:T(8,128)S(1)} custom-call(f32[1,128,128]{2,1,0:T(8,128)S(1)} %cholesky.604), custom_call_target="Cholesky" | custom-call | tf_op jit(solution)/shard_map/jit(cholesky)/cholesky | solution.py:72
  333.9 0.6 select_reduce_fusion.3
  334.6 9.8 %custom-call.76 = f32[1,1,128,128]{2,3,1,0:T(8,128)S(1)} custom-call(f32[1,1,128,128]{3,2,1,0:T(8,128)S(1)} %get-tuple-element.12), custom_call_target="InvertDiagBlocksLowerTriangular" | custom-call | tf_op jit(solution)/shard_map/jit(cholesky)/cholesky | solution.py:72
  344.4 1.3 fusion.12
  345.7 2.3 fusion.13
  348.0 11.7 %custom-call.77 = f32[1,128,128]{2,1,0:T(8,128)S(1)} custom-call(f32[1,128,128]{2,1,0:T(8,128)S(1)} %cholesky.609), custom_call_target="Cholesky" | custom-call | tf_op jit(solution)/shard_map/jit(cholesky)/cholesky | solution.py:72
  359.7 0.6 select_reduce_fusion.2
  360.3 9.8 %custom-call.78 = f32[1,1,128,128]{2,3,1,0:T(8,128)S(1)} custom-call(f32[1,1,128,128]{3,2,1,0:T(8,128)S(1)} %get-tuple-element.9), custom_call_target="InvertDiagBlocksLowerTriangular" | custom-call | tf_op jit(solution)/shard_map/jit(cholesky)/cholesky | solution.py:72
  370.1 0.9 fusion.14
  371.0 2.0 fusion.15
  373.1 11.7 %custom-call.79 = f32[1,128,128]{2,1,0:T(8,128)S(1)} custom-call(f32[1,128,128]{2,1,0:T(8,128)S(1)} %cholesky.614), custom_call_target="Cholesky" | custom-call | tf_op jit(solution)/shard_map/jit(cholesky)/cholesky | solution.py:72
  384.8 0.6 select_reduce_fusion.1
  385.5 10.2 %custom-call.80 = f32[1,1,128,128]{2,3,1,0:T(8,128)S(1)} custom-call(f32[1,1,128,128]{3,2,1,0:T(8,128)S(1)} %get-tuple-element.6), custom_call_target="InvertDiagBlocksLowerTriangular" | custom-call | tf_op jit(solution)/shard_map/jit(cholesky)/cholesky | solution.py:72
  395.6 0.8 fusion.16
  396.5 1.8 fusion.17
  398.3 11.7 %custom-call.81 = f32[1,128,128]{2,1,0:T(8,128)S(1)} custom-call(f32[1,128,128]{2,1,0:T(8,128)S(1)} %fusion.17), custom_call_target="Cholesky" | custom-call | tf_op jit(solution)/shard_map/jit(cholesky)/cholesky | solution.py:72
  410.0 0.6 select_reduce_fusion
  410.6 0.7 compare_reduce_fusion.5
  411.3 0.6 compare_reduce_fusion.4
  411.9 0.7 compare_reduce_fusion.3
  412.6 0.7 compare_reduce_fusion.2
  413.3 0.7 compare_reduce_fusion.1
  414.0 0.6 compare_reduce_fusion
  414.6 0.6 compare_reduce_fusion.6
  420.3 30.2 %multiply_convert_fusion.1.clone.4 = bf16[512,4096]{1,0:T(8,128)(2,1)S(1)} fusion(bf16[4096,256]{1,0:T(8,128)(2,1)S(1)} %copy-done.6, f32[512]{0:T(512)S(1)} %dynamic_slice.21, bf16[256,8192]{1,0:T(8,128)(2,1)} %all-gather.7.cloned.1.call-done, s32[]{:T(128)S(6)} %select_n.29), kind=kOutput, calls=%fused_computation.1.clone.clone.clone.1 | convolution fusion | flops 1080033280 | bytes 6555652 | tf_op jit(solution)/shard_map/dot_general | solution.py:12
  450.5 3.4 convolution_add_fusion
  453.9 1.6 fusion.4
  (26 shorter events, 0.2 us)
Async XLA Ops:
  7.2 69.7 %all-gather.5.cloned.1.call-start = ((), (), s32[]{:S(2)}) async-start(), calls=%async_computation | async-start | bytes 2228224 | tf_op jit(solution)/shard_map/all_gather | solution.py:42
  7.9 106.6 %all-gather.7.cloned.1.call-start = ((), (), s32[]{:S(2)}) async-start(), calls=%async_computation.1 | async-start | bytes 4456448 | tf_op jit(solution)/shard_map/all_gather | solution.py:46
  106.3 2.0 copy-start.3
  108.3 6.2 %copy-start.6 = (bf16[4096,256]{1,0:T(8,128)(2,1)S(1)}, bf16[4096,256]{1,0:T(8,128)(2,1)}, u32[]{:S(2)}) copy-start(bf16[4096,256]{1,0:T(8,128)(2,1)} %all-gather.5.cloned.1.call-done) | copy-start | bytes 6291460
  201.0 1.9 copy-start.1
  214.9 1.9 copy-start.2
  420.3 30.2 %copy-start.4 = (bf16[4096,512]{1,0:T(8,128)(2,1)S(1)}, bf16[4096,512]{1,0:T(8,128)(2,1)}, u32[]{:S(2)}) copy-start(bf16[4096,512]{1,0:T(8,128)(2,1)} %copy-done.3) | copy-start | bytes 12582916
  420.3 30.2 %copy-start.5 = (f32[512]{0:T(512)S(1)}, f32[512]{0:T(512)}, u32[]{:S(2)}) copy-start(f32[512]{0:T(512)} %param.8) | copy-start | bytes 6148
  450.5 3.4 copy-start
Sparse Core Ops, SparseCore 0:
  9.8 43.6 all-gather.4
  55.9 58.5 all-gather.6
where the time goes:
time: 472 us; the launch traced here: 463 us
  other arithmetic  181 us (38%)
  matrix products  174 us (37%)
  blocking collectives  68.1 us (14%)
  between operations  19.6 us (4%)
  local copies, waits for them, and re-layouts  13.8 us (3%)
  waiting for transfers between devices  6.32 us (1%)
    another operation x30, other arithmetic, shards(): factors_all = jnp.linalg.cholesky(stacked).reshape(window, FB)  172 us
    dot_general x3, matrix products, features(): jnp.dot(rows, freq_cols, preferred_element_type=jnp.float32) + phase_cols  119 us
    all_gather x1, blocking collectives, shards(): lax.all_gather(targets, 'dp', axis=1, tiled=True)  30.9 us
    dot_general x2, matrix products, cross(): lax.dot_general(left, right, (((0,), (0,)), ((), ())), preferred_element_...  30.1 us
    another operation x14, matrix products, shards(): factors_all = jnp.linalg.cholesky(stacked).reshape(window, FB)  23.3 us
    all_gather x1, blocking collectives, shards(): lax.all_gather(phase, 'feat', axis=0, tiled=True)  19.1 us
    all_gather x1, blocking collectives, shards(): lax.all_gather(ridge, 'feat', axis=0, tiled=True)  18 us
  transfers between devices with their start and end apart: 2, of which 1 were waited for; matrix products, arithmetic and copies ran while one was open for 7% of the time, Pallas kernels for 0%

commit v1 on v0

v1 whole, which is shorter than its diff:
```python
import functools
import math

import jax
import jax.numpy as jnp
from jax import lax
from jax.experimental import pallas as pl
from jax.experimental.pallas import tpu as pltpu
from jax.sharding import PartitionSpec as P

FB = 1024
NB = 128
HI = lax.Precision.HIGHEST
TURN = 1.0 / (2.0 * math.pi)
C1, C3, C5, C7 = -6.283164044054801, 41.33714233314145, -81.34076747300007, 70.99341851060123


def cos_turns(turns, scale):
    r = turns - jnp.round(turns)
    u = jnp.abs(r) - 0.25
    w = u * u
    poly = ((C7 * scale * w + C5 * scale) * w + C3 * scale) * w + C1 * scale
    return poly * u


def tdot(left, right, precision=None):
    return lax.dot_general(
        left, right, (((0,), (0,)), ((), ())), precision=precision, preferred_element_type=jnp.float32
    )


def row_of(x, r):
    return jnp.broadcast_to(x[r:r + 1, :], x.shape)


def lane_of(x, c):
    return jnp.broadcast_to(x[:, c:c + 1], x.shape)


def leaf(blocks):
    n = NB // 8
    sub = lax.broadcasted_iota(jnp.int32, (8, NB), 0)
    lane = lax.broadcasted_iota(jnp.int32, (8, NB), 1)
    a = list(blocks)
    e = [jnp.where(lane == sub + 8 * m, 1.0, 0.0).astype(jnp.float32) for m in range(n)]
    outs = []
    for k in range(n):
        pa, pe = a[k], e[k]
        v = [lane_of(pa, 8 * k + c) for c in range(8)]
        cols = {m: [lane_of(a[m], 8 * k + c) for c in range(8)] for m in range(k + 1, n)}
        nxt = k + 1 < n
        if nxt:
            na, ne = a[k + 1], e[k + 1]
            nv = list(cols[k + 1])
        rs = jnp.zeros((8, NB), jnp.float32)
        dv = jnp.zeros((8, NB), jnp.float32)
        for r in range(8):
            d = row_of(v[r], r)
            inv = 1.0 / d
            rs = jnp.where(sub == r, lax.rsqrt(d), rs)
            dv = jnp.where(sub == r, inv, dv)
            l = jnp.where(sub > r, v[r] * inv, 0.0)
            ba, be = row_of(pa, r), row_of(pe, r)
            if nxt:
                l1 = nv[r] * inv
                na = na - l1 * ba
                ne = ne - l1 * be
            pa = pa - l * ba
            pe = pe - l * be
            for c in range(r + 1, 8):
                b = row_of(v[c], r)
                v[c] = v[c] - l * b
                if nxt:
                    nv[c] = nv[c] - l1 * b
        outs.append((pa * rs, pe * rs))
        if nxt:
            a[k + 1], e[k + 1] = na, ne
        if k + 2 < n:
            qa, qe = pa * dv, pe * dv
            for r in range(7, 0, -1):
                mult = jnp.where(sub < r, v[r] * dv, 0.0)
                qa = qa - mult * row_of(qa, r)
                qe = qe - mult * row_of(qe, r)
            ra = [row_of(qa, r) for r in range(8)]
            re = [row_of(qe, r) for r in range(8)]
            for m in range(k + 2, n):
                ma = [cols[m][r] * ra[r] for r in range(8)]
                me = [cols[m][r] * re[r] for r in range(8)]
                while len(ma) > 1:
                    ma = [ma[i] + ma[i + 1] for i in range(0, len(ma), 2)]
                    me = [me[i] + me[i + 1] for i in range(0, len(me), 2)]
                a[m] = a[m] - ma[0]
                e[m] = e[m] - me[0]
    return outs


def kernel(scale, feat_axis, data_axis, pts, tgt, fw, fd, phw, phd, rdg, gram, proj, fac, wphi, cphi, slab, ue, own_phi):
    rows = pts.shape[0]
    half = fd.shape[1]
    feat = lax.axis_index(feat_axis)
    data = lax.axis_index(data_axis)
    odd = lax.rem(feat, FB // half)
    own = pl.multiple_of(odd * half, half)

    def chunk(i, _):
        at = pl.ds(pl.multiple_of(i * 256, 256), 256)
        p = pts[at, :]
        for src, ph, dst, width in ((fw, phw, wphi, FB), (fd, phd, cphi, half)):
            for j in range(0, width, 256):
                ang = jnp.dot(p, src[:, j:j + 256], preferred_element_type=jnp.float32)
                dst[at, j:j + 256] = cos_turns(ang * TURN + ph[:, j:j + 256], scale).astype(jnp.bfloat16)
        return 0

    lax.fori_loop(0, rows // 256, chunk, 0)

    own_phi[...] = wphi[:, pl.ds(own, half)]
    proj[...] = jnp.dot(tgt[...], own_phi[...], preferred_element_type=jnp.float32)
    gram[...] = tdot(own_phi[...], cphi[...])

    def eye_add(ref, row0, rvec):
        n = rvec.shape[1]
        for i in range(0, n, NB):
            eye = lax.broadcasted_iota(jnp.int32, (NB, NB), 0) == lax.broadcasted_iota(jnp.int32, (NB, NB), 1)
            ref[row0 + i:row0 + i + NB, i:i + NB] += jnp.where(eye, rvec[:, i:i + NB], 0.0)

    @pl.when(feat == data)
    def _():
        eye_add(gram, 0, rdg[:, pl.ds(own, half)])

    slab[0:512, :] = tdot(wphi[:, 0:512], wphi[...])
    slab[512:1024, 512:1024] = tdot(wphi[:, 512:1024], wphi[:, 512:1024])
    eye_add(slab, 0, rdg[...])

    nblk = FB // NB

    def step(k, _):
        at = pl.multiple_of(k * NB, NB)
        blocks = [slab[pl.ds(pl.multiple_of(at + 8 * m, 8), 8), pl.ds(at, NB)] for m in range(NB // 8)]
        sub = lax.broadcasted_iota(jnp.int32, (8, NB), 0)
        lane = lax.broadcasted_iota(jnp.int32, (8, NB), 1)
        for m, (u, x) in enumerate(leaf(blocks)):
            slab[pl.ds(pl.multiple_of(at + 8 * m, 8), 8), pl.ds(at, NB)] = jnp.where(lane >= sub + 8 * m, u, 0.0)
            ue[8 * m:8 * m + 8, :] = x
        for kk in range(nblk - 1):
            @pl.when(k == kk)
            def _():
                lo, mid = kk * NB, (kk + 1) * NB
                u12 = jnp.dot(ue[...], slab[lo:mid, mid:], precision=HI, preferred_element_type=jnp.float32)
                slab[lo:mid, mid:] = u12
                for i in range(mid, FB, 256):
                    w = min(256, FB - i)
                    slab[i:i + w, i:] -= tdot(u12[:, i - mid:i - mid + w], u12[:, i - mid:], HI)
        return 0

    lax.fori_loop(0, nblk, step, 0)

    for b in range(half // NB):
        for j in range(nblk):
            piece = jnp.transpose(slab[j * NB:(j + 1) * NB, pl.ds(pl.multiple_of(own + b * NB, NB), NB)])
            keep = j * NB <= own + b * NB
            fac[b * NB:(b + 1) * NB, j * NB:(j + 1) * NB] = jnp.where(keep, piece, 0.0)


def local(scale, pts, tgt, fw, fd, phw, phd, rdg, interpret=False):
    rows, half = pts.shape[0], fd.shape[1]
    f32 = jnp.float32
    return pl.pallas_call(
        functools.partial(kernel, scale, "feat", "dp"),
        out_shape=(
            jax.ShapeDtypeStruct((half, half), f32),
            jax.ShapeDtypeStruct((8, half), f32),
            jax.ShapeDtypeStruct((half, FB), f32),
        ),
        scratch_shapes=[
            pltpu.VMEM((rows, FB), jnp.bfloat16),
            pltpu.VMEM((rows, half), jnp.bfloat16),
            pltpu.VMEM((FB, FB), f32),
            pltpu.VMEM((NB, NB), f32),
            pltpu.VMEM((rows, half), jnp.bfloat16),
        ],
        compiler_params=pltpu.CompilerParams(vmem_limit_bytes=60 * 1024 * 1024),
        interpret=interpret,
    )(pts, tgt, fw, fd, phw, phd, rdg)


def shards(points, freqs, phase, ridge, targets):
    data_count = lax.axis_size("dp")
    feat_count = lax.axis_size("feat")
    feat = lax.axis_index("feat")
    rows = points.shape[0]
    half = freqs.shape[1]
    scale = math.sqrt(2.0 / (rows * data_count))
    pack = lax.all_gather(jnp.concatenate([points, targets], 0), "dp", axis=0)
    points_all = pack[:, :rows].reshape(rows * data_count, -1)
    targets_all = jnp.transpose(pack[:, rows:], (1, 0, 2)).reshape(targets.shape[0], -1)
    small = jnp.stack([phase * TURN, ridge])
    pair = [(i, i ^ 1) for i in range(feat_count)]
    swap = [(d * feat_count + f, f * feat_count + d) for d in range(data_count) for f in range(feat_count)]
    f_other, s_other = lax.ppermute(freqs, "feat", pair), lax.ppermute(small, "feat", pair)
    f_tile, s_tile = lax.ppermute(freqs, ("dp", "feat"), swap), lax.ppermute(small, ("dp", "feat"), swap)
    odd = lax.rem(feat, 2) == 1
    fw = jnp.where(odd, jnp.concatenate([f_other, freqs], 1), jnp.concatenate([freqs, f_other], 1))
    sw = jnp.where(odd, jnp.concatenate([s_other, small], 1), jnp.concatenate([small, s_other], 1))
    return local(scale, points_all, targets_all, fw, f_tile, sw[0:1], s_tile[0:1], sw[1:2])


def solution(mesh):
    in_specs = (P("dp", None), P(None, "feat"), P("feat"), P("feat"), P(None, "dp"))
    out_specs = (P("feat", "dp"), P(None, "feat"), P("feat", None))
    return jax.shard_map(shards, mesh=mesh, in_specs=in_specs, out_specs=out_specs, check_vma=False)
```

time: 472 us -> 155 us (0.33); the launches traced: 463 us -> 154 us
  other arithmetic: 181 us -> 5.71 us
  matrix products: 174 us -> 0 us
  Pallas kernels: 0 us -> 73 us
  blocking collectives: 68.1 us -> 0 us
  waiting for transfers between devices: 6.32 us -> 46 us
  starting transfers between devices: 0.08 us -> 8.78 us
  local copies, waits for them, and re-layouts: 13.8 us -> 6.46 us
  between operations: 19.6 us -> 14.1 us
    another operation x31 -> x1, other arithmetic: 175 us -> 0.69 us  [shards(): small = jnp.stack([phase * TURN, ridge])]
    dot_general x6 -> x0, matrix products: 151 us -> none  [the longest x3 119 us: features(): jnp.dot(rows, freq_cols, preferred_element_type=jnp.float32) + phase_cols]
    pallas_call x0 -> x1, Pallas kernels: none -> 73 us  [local(): pl.pallas_call(functools.partial(kernel, scale, 'feat', 'dp'), out_shape=...]
    all_gather x3 -> x0, blocking collectives: 68.1 us -> none  [the longest x1 30.9 us: shards(): lax.all_gather(targets, 'dp', axis=1, tiled=True)]
    all_gather x2 -> x1, waiting for transfers between devices: 4.95 us -> 40.1 us  [shards(): pack = lax.all_gather(jnp.concatenate([points, targets], 0), 'dp', axis=0)]
    another operation x14 -> x0, matrix products: 23.3 us -> none  [shards(): factors_all = jnp.linalg.cholesky(stacked).reshape(window, FB)]
    ppermute x0 -> x4, starting transfers between devices: none -> 8.75 us  [the longest x1 4.61 us: shards(): lax.ppermute(small, ('dp', 'feat'), swap)]
    another operation x9 -> x0, local copies, waits for them, and re-layouts: 7.89 us -> none  [the longest x1 5.34 us: shards(): stacked = jnp.stack([slab])]
  transfers between devices with their start and end apart: 2 -> 5, of which waited for: 1 -> 2; matrix products, arithmetic and copies ran while one was open for 7% -> 6% of each run, Pallas kernels for 0% -> 0%
where the time goes in v1:
time: 155 us; the launch traced here: 154 us
  Pallas kernels  73 us (47%)
  waiting for transfers between devices  46 us (30%)
  between operations  14.1 us (9%)
  starting transfers between devices  8.78 us (6%)
  local copies, waits for them, and re-layouts  6.46 us (4%)
  other arithmetic  5.71 us (4%)
    pallas_call x1, Pallas kernels, local(): pl.pallas_call(functools.partial(kernel, scale, 'feat', 'dp'), out_shape=...  73 us
    all_gather x1, waiting for transfers between devices, shards(): pack = lax.all_gather(jnp.concatenate([points, targets], 0), 'dp', axis=0)  40.1 us
    ppermute x1, waiting for transfers between devices, shards(): lax.ppermute(freqs, 'feat', pair)  5.86 us
    ppermute x1, starting transfers between devices, shards(): lax.ppermute(small, ('dp', 'feat'), swap)  4.61 us
  transfers between devices with their start and end apart: 5, of which 2 were waited for; matrix products, arithmetic and copies ran while one was open for 6% of the time, Pallas kernels for 0%

profile of v1, /device:TPU:1, one launch (start us, length us, event | category | flops | bytes accessed | tf_op | source)
XLA Modules:
  0.0 154.0 jit_solution(10231555714887443153)
XLA Ops:
  7.2 0.0 all-gather.3.cloned.1.call-start
  7.2 1.6 %pad_maximum_fusion = bf16[264,256]{1,0:T(8,128)(2,1)} fusion(bf16[8,256]{1,0:T(8,128)(2,1)} %param.9, bf16[256,256]{1,0:T(8,128)(2,1)} %param.5), kind=kLoop, calls=%fused_computation.1 | loop fusion | flops 270336 | bytes 270336 | tf_op jit(solution)/shard_map/concatenate | solution.py:193
  8.8 0.0 all-gather.3.cloned.1.call-update
  8.8 0.7 broadcast_multiply_fusion
  9.5 0.7 pad_maximum_fusion.1
  10.2 2.1 %collective-permute-start.2 = (f32[2,512]{1,0:T(2,128)S(1)}, f32[2,512]{1,0:T(2,128)S(1)}, u32[]{:S(2)}, u32[]{:S(2)}) collective-permute-start(f32[2,512]{1,0:T(2,128)S(1)} %pad_maximum_fusion.1), channel_id=1, source_target_pairs={{0,1},{1,0},{2,3},{3,2},{4,5},{5,4},{6,7},{7,6},{8,9},{9,8},{10,11... | collective-permute-start | bytes 12296 | tf_op jit(solution)/shard_map/ppermute | solution.py:199
  12.3 4.6 %collective-permute-start.3 = (f32[2,512]{1,0:T(2,128)S(1)}, f32[2,512]{1,0:T(2,128)S(1)}, u32[]{:S(2)}, u32[]{:S(2)}) collective-permute-start(f32[2,512]{1,0:T(2,128)S(1)} %pad_maximum_fusion.1), channel_id=1, source_target_pairs={{0,0},{1,16},{2,32},{3,48},{4,64},{5,80},{6,96},{7,112},{8,128},{9... | collective-permute-start | bytes 12296 | tf_op jit(solution)/shard_map/ppermute | solution.py:200
  16.9 0.1 collective-permute-start
  17.0 1.9 %collective-permute-start.1 = (bf16[256,512]{1,0:T(8,128)(2,1)}, bf16[256,512]{1,0:T(8,128)(2,1)S(1)}, u32[]{:S(2)}, u32[]{:S(2)}) collective-permute-start(bf16[256,512]{1,0:T(8,128)(2,1)} %param.6), channel_id=1, source_target_pairs={{0,0},{1,16},{2,32},{3,48},{4,64},{5,80},{6,96},{7,112},{8,128},{9... | collective-permute-start | bytes 786440 | tf_op jit(solution)/shard_map/ppermute | solution.py:200
  19.0 0.0 collective-permute-done.2
  19.0 0.8 maximum_select_fusion.1
  19.8 0.0 collective-permute-done.3
  19.8 0.6 slice.23.phd
  20.4 0.6 fusion
  21.0 5.9 %collective-permute-done = bf16[256,512]{1,0:T(8,128)(2,1)S(1)} collective-permute-done((bf16[256,512]{1,0:T(8,128)(2,1)}, bf16[256,512]{1,0:T(8,128)(2,1)S(1)}, u32[]{:S(2)}, u32[]{:S(2)}) %collective-permute-start) | collective-permute-done | bytes 262176 | tf_op jit(solution)/shard_map/ppermute | solution.py:199
  26.8 2.0 %maximum_select_fusion.fw = bf16[256,1024]{1,0:T(8,128)(2,1)} fusion(bf16[256,512]{1,0:T(8,128)(2,1)} %param.6, bf16[256,512]{1,0:T(8,128)(2,1)S(1)} %collective-permute-done, pred[]{:T(512)S(6)} %eq.3), kind=kLoop, calls=%fused_computation | loop fusion | flops 2359296 | bytes 1048577 | tf_op jit(solution)/shard_map/jit(_where)/select_n | solution.py:202
  28.8 40.1 %all-gather.3.cloned.1.call-done = bf16[4224,256]{1,0:T(8,128)(2,1)} async-done(((bf16[264,256]{1,0:T(8,128)(2,1)}), bf16[4224,256]{1,0:T(8,128)(2,1)}) %all-gather.3.cloned.1.call-update) | async-done | bytes 2162704 | tf_op jit(solution)/shard_map/all_gather | solution.py:193
  68.9 1.5 slice.21
  70.4 3.1 %slice.20 = bf16[16,256,256]{2,1,0:T(8,128)(2,1)} slice(bf16[16,264,256]{2,1,0:T(8,128)(2,1)} %bitcast.9), slice={[0:16], [0:256], [0:256]} | slice | bytes 4194304 | tf_op jit(solution)/shard_map/slice | solution.py:194
  73.5 0.0 collective-permute-done.1.fd
  73.5 0.0 copy-start
  73.5 0.7 copy-done
  74.2 73.0 %shard_map.76 = (f32[512,512]{1,0:T(8,128)}, f32[8,512]{1,0:T(8,128)}, f32[512,1024]{1,0:T(8,128)}) custom-call(bf16[4096,256]{1,0:T(8,128)(2,1)} %bitcast.7, bf16[8,4096]{1,0:T(8,128)(2,1)} %bitcast.10, bf16[256,1024]{1,0:T(8,128)(2,1)} %maximum_select_fusion.fw, bf16[256,512]{1,0:T(8,128)(2,1)} %copy-done, f32[1,1024]{1,0:T(1,128)} %get-tuple-element.4.phw, ...), custom_call_target="tpu_custom_call" | custom-call | tf_op jit(solution)/shard_map/pallas_call | solution.py:167
Async XLA Ops:
  7.2 61.8 %all-gather.3.cloned.1.call-start = ((), (), s32[]{:S(2)}) async-start(), calls=%async_computation | async-start | bytes 2297856 | tf_op jit(solution)/shard_map/all_gather | solution.py:193
  10.2 8.8 %collective-permute-start.2 = (f32[2,512]{1,0:T(2,128)S(1)}, f32[2,512]{1,0:T(2,128)S(1)}, u32[]{:S(2)}, u32[]{:S(2)}) collective-permute-start(f32[2,512]{1,0:T(2,128)S(1)} %pad_maximum_fusion.1), channel_id=1, source_target_pairs={{0,1},{1,0},{2,3},{3,2},{4,5},{5,4},{6,7},{7,6},{8,9},{9,8},{10,11... | collective-permute-start | bytes 12296 | tf_op jit(solution)/shard_map/ppermute | solution.py:199
  12.3 7.4 %collective-permute-start.3 = (f32[2,512]{1,0:T(2,128)S(1)}, f32[2,512]{1,0:T(2,128)S(1)}, u32[]{:S(2)}, u32[]{:S(2)}) collective-permute-start(f32[2,512]{1,0:T(2,128)S(1)} %pad_maximum_fusion.1), channel_id=1, source_target_pairs={{0,0},{1,16},{2,32},{3,48},{4,64},{5,80},{6,96},{7,112},{8,128},{9... | collective-permute-start | bytes 12296 | tf_op jit(solution)/shard_map/ppermute | solution.py:200
  16.9 9.9 %collective-permute-start = (bf16[256,512]{1,0:T(8,128)(2,1)}, bf16[256,512]{1,0:T(8,128)(2,1)S(1)}, u32[]{:S(2)}, u32[]{:S(2)}) collective-permute-start(bf16[256,512]{1,0:T(8,128)(2,1)} %param.6), channel_id=1, source_target_pairs={{0,1},{1,0},{2,3},{3,2},{4,5},{5,4},{6,7},{7,6},{8,9},{9,8},{10,11... | collective-permute-start | bytes 786440 | tf_op jit(solution)/shard_map/ppermute | solution.py:199
  17.0 56.5 %collective-permute-start.1 = (bf16[256,512]{1,0:T(8,128)(2,1)}, bf16[256,512]{1,0:T(8,128)(2,1)S(1)}, u32[]{:S(2)}, u32[]{:S(2)}) collective-permute-start(bf16[256,512]{1,0:T(8,128)(2,1)} %param.6), channel_id=1, source_target_pairs={{0,0},{1,16},{2,32},{3,48},{4,64},{5,80},{6,96},{7,112},{8,128},{9... | collective-permute-start | bytes 786440 | tf_op jit(solution)/shard_map/ppermute | solution.py:200
  73.5 0.7 copy-start
Sparse Core Ops, SparseCore 0:
  10.4 58.5 all-gather.2

commit v2 on v1

--- a/solution.py
+++ b/solution.py
@@ -10,9 +10,181 @@
 
 FB = 1024
 NB = 128
+XS = 4
+YS = 4
+ZS = 8
 HI = lax.Precision.HIGHEST
+MESH = pl.DeviceIdType.MESH
 TURN = 1.0 / (2.0 * math.pi)
 C1, C3, C5, C7 = -6.283164044054801, 41.33714233314145, -81.34076747300007, 70.99341851060123
+
+
+def exchange(pack, freqs, small, points, other_f, other_s, tile_f, tile_s,
+             up_send, up_recv, dn_send, dn_recv, mate_send, mate_recv,
+             pair_send, pair_recv, tree_recv, row_send, col_send, local_sem):
+    data, feat = lax.axis_index("dp"), lax.axis_index("feat")
+    z, core = data // 2, data % 2
+    x, y = feat // YS, feat % YS
+    first = 128
+
+    def at(zz, cc):
+        return {"dp": zz * 2 + cc, "feat": feat}
+
+    def near(xx, yy):
+        return {"dp": data, "feat": xx * YS + yy}
+
+    up, dn = (z + 1) % ZS, (z + ZS - 1) % ZS
+    barrier = pltpu.get_barrier_semaphore()
+    peers = [at(up, core), at(dn, core), at(z, 1 - core)]
+    peers += [near((x + i) % XS, y) for i in range(1, XS)] + [near(x, (y + i) % YS) for i in range(1, YS)]
+    for peer in peers:
+        pl.semaphore_signal(barrier, inc=1, device_id=peer, device_id_type=MESH)
+    pl.semaphore_wait(barrier, len(peers))
+
+    pieces = (pl.ds(0, first), pl.ds(first, pack.shape[0] - first))
+
+    def remote(src, dst, ssem, rsem, where):
+        return pltpu.make_async_remote_copy(
+            src_ref=src, dst_ref=dst, send_sem=ssem, recv_sem=rsem, device_id=where, device_id_type=MESH)
+
+    sends = []
+
+    def go(copy):
+        copy.start()
+        sends.append(copy)
+        return copy
+
+    def slot(zz):
+        return ((zz + 2 * ZS) % ZS) * 2 + core
+
+    def ring(step, p, upward):
+        zz = z - step if upward else z + step
+        src = pack.at[pieces[p]] if step == 0 else points.at[slot(zz), pieces[p]]
+        dst = points.at[slot(zz), pieces[p]]
+        if upward:
+            return remote(src, dst, up_send.at[step, p], up_recv.at[step, p], at(up, core))
+        return remote(src, dst, dn_send.at[step, p], dn_recv.at[step, p], at(dn, core))
+
+    def mate(i, p, zz, own=False):
+        src = pack.at[pieces[p]] if own else points.at[slot(zz), pieces[p]]
+        return remote(src, points.at[slot(zz), pieces[p]], mate_send.at[i, p], mate_recv.at[i, p], at(z, 1 - core))
+
+    for p in range(2):
+        go(ring(0, p, True))
+        go(ring(0, p, False))
+    pair_y = y + 1 - 2 * (y % 2)
+    pair_copies = [
+        remote(small, other_s, pair_send.at[0], pair_recv.at[0], near(x, pair_y)),
+        remote(freqs, other_f, pair_send.at[1], pair_recv.at[1], near(x, pair_y)),
+    ]
+    for copy in pair_copies:
+        go(copy)
+    keep = pltpu.make_async_copy(pack, points.at[slot(z)], local_sem.at[0])
+    keep.start()
+    for p in range(2):
+        go(mate(0, p, z, own=True))
+
+    rx, ry = data // YS, data % YS
+    parts = [(small, tile_s, None), (freqs, tile_f, pl.ds(0, 128)), (freqs, tile_f, pl.ds(128, 128))]
+
+    def part(ref, cut):
+        return ref if cut is None else ref.at[cut]
+
+    def to_row(n, i):
+        src, dst, cut = parts[n]
+        return remote(part(src, cut), part(dst, cut), row_send.at[n, i], tree_recv.at[n], near((x + i + 1) % XS, y))
+
+    def to_col(n, i, own):
+        src, dst, cut = parts[n]
+        return remote(part(src if own else dst, cut), part(dst, cut), col_send.at[n, i], tree_recv.at[n],
+                      near(x, (y + i + 1) % YS))
+
+    root = jnp.logical_and(x == rx, y == ry)
+    mid = jnp.logical_and(x != rx, y == ry)
+
+    @pl.when(root)
+    def _():
+        for n in range(3):
+            for i in range(XS - 1):
+                to_row(n, i).start()
+            for i in range(YS - 1):
+                to_col(n, i, True).start()
+        a = pltpu.make_async_copy(freqs, tile_f, local_sem.at[1])
+        b = pltpu.make_async_copy(small, tile_s, local_sem.at[2])
+        a.start()
+        b.start()
+        a.wait()
+        b.wait()
+
+    def pass_on(n):
+        @pl.when(mid)
+        def _():
+            to_row(n, 0).wait_recv()
+            for i in range(YS - 1):
+                to_col(n, i, False).start()
+
+    for step in range(1, 5):
+        todo = [(0, True), (0, False), (1, True), (1, False)] if step < 4 else [(0, True), (1, False)]
+        for p, upward in todo:
+            ring(step - 1, p, upward).wait_recv()
+            if step < 3 or (step == 3 and p == (0 if upward else 1)):
+                go(ring(step, p, upward))
+            go(mate(2 * step - 1 + (0 if upward or step == 4 else 1), p, z - step if upward else z + step))
+        if step == 1:
+            pass_on(0)
+            pass_on(1)
+        if step == 2:
+            pass_on(2)
+
+    @pl.when(y != ry)
+    def _():
+        for n in range(3):
+            to_col(n, 0, False).wait_recv()
+
+    for i in range(8):
+        for p in range(2):
+            mate(i, p, z).wait_recv()
+    for copy in pair_copies:
+        copy.wait_recv()
+    keep.wait()
+
+    @pl.when(root)
+    def _():
+        for n in range(3):
+            for i in range(XS - 1):
+                to_row(n, i).wait_send()
+
+    @pl.when(y == ry)
+    def _():
+        for n in range(3):
+            for i in range(YS - 1):
+                to_col(n, i, False).wait_send()
+
+    for copy in sends:
+        copy.wait_send()
+
+
+def gather(pack, freqs, small):
+    dma = pltpu.SemaphoreType.DMA
+    vmem = pl.BlockSpec(memory_space=pltpu.VMEM)
+    shape = jax.ShapeDtypeStruct
+    return pl.pallas_call(
+        exchange,
+        out_shape=(
+            shape((2 * ZS,) + pack.shape, pack.dtype),
+            shape(freqs.shape, freqs.dtype),
+            shape(small.shape, small.dtype),
+            shape(freqs.shape, freqs.dtype),
+            shape(small.shape, small.dtype),
+        ),
+        in_specs=[vmem] * 3,
+        out_specs=(vmem,) * 5,
+        scratch_shapes=[
+            dma((4, 2)), dma((4, 2)), dma((4, 2)), dma((4, 2)), dma((8, 2)), dma((8, 2)),
+            dma((2,)), dma((2,)), dma((3,)), dma((3, 3)), dma((3, 3)), dma((3,)),
+        ],
+        compiler_params=pltpu.CompilerParams(collective_id=0, has_side_effects=True),
+    )(pack, freqs, small)
 
 
 def cos_turns(turns, scale):
@@ -94,42 +266,46 @@
     return outs
 
 
-def kernel(scale, feat_axis, data_axis, pts, tgt, fw, fd, phw, phd, rdg, gram, proj, fac, wphi, cphi, slab, ue, own_phi):
-    rows = pts.shape[0]
+def kernel(scale, feat_axis, data_axis, pts, fo, fp, fd, so, sp, sd, gram, proj, fac, wphi, cphi, slab, ue, own_phi, tgt):
+    count = pts.shape[0]
     half = fd.shape[1]
+    block = 256
     feat = lax.axis_index(feat_axis)
     data = lax.axis_index(data_axis)
     odd = lax.rem(feat, FB // half)
     own = pl.multiple_of(odd * half, half)
+    oth = pl.multiple_of((1 - odd) * half, half)
 
     def chunk(i, _):
-        at = pl.ds(pl.multiple_of(i * 256, 256), 256)
-        p = pts[at, :]
-        for src, ph, dst, width in ((fw, phw, wphi, FB), (fd, phd, cphi, half)):
-            for j in range(0, width, 256):
+        at = pl.ds(pl.multiple_of(i * block, block), block)
+        p = pts[i, 0:block, :]
+        for src, sm, dst, base in ((fo, so, wphi, own), (fp, sp, wphi, oth), (fd, sd, cphi, 0)):
+            for j in range(0, half, 256):
                 ang = jnp.dot(p, src[:, j:j + 256], preferred_element_type=jnp.float32)
-                dst[at, j:j + 256] = cos_turns(ang * TURN + ph[:, j:j + 256], scale).astype(jnp.bfloat16)
+                to = pl.ds(pl.multiple_of(base + j, 256), 256)
+                dst[at, to] = cos_turns(ang * TURN + sm[0:1, j:j + 256] * TURN, scale).astype(jnp.bfloat16)
         return 0
 
-    lax.fori_loop(0, rows // 256, chunk, 0)
-
+    lax.fori_loop(0, count, chunk, 0)
+
+    for i in range(count):
+        tgt[:, i * block:(i + 1) * block] = pts[i, block:block + 8, :]
     own_phi[...] = wphi[:, pl.ds(own, half)]
     proj[...] = jnp.dot(tgt[...], own_phi[...], preferred_element_type=jnp.float32)
     gram[...] = tdot(own_phi[...], cphi[...])
-
-    def eye_add(ref, row0, rvec):
-        n = rvec.shape[1]
-        for i in range(0, n, NB):
-            eye = lax.broadcasted_iota(jnp.int32, (NB, NB), 0) == lax.broadcasted_iota(jnp.int32, (NB, NB), 1)
-            ref[row0 + i:row0 + i + NB, i:i + NB] += jnp.where(eye, rvec[:, i:i + NB], 0.0)
+    eye = lax.broadcasted_iota(jnp.int32, (NB, NB), 0) == lax.broadcasted_iota(jnp.int32, (NB, NB), 1)
 
     @pl.when(feat == data)
     def _():
-        eye_add(gram, 0, rdg[:, pl.ds(own, half)])
+        for i in range(0, half, NB):
+            gram[i:i + NB, i:i + NB] += jnp.where(eye, so[1:2, i:i + NB], 0.0)
 
     slab[0:512, :] = tdot(wphi[:, 0:512], wphi[...])
     slab[512:1024, 512:1024] = tdot(wphi[:, 512:1024], wphi[:, 512:1024])
-    eye_add(slab, 0, rdg[...])
+    for sm, base in ((so, own), (sp, oth)):
+        for i in range(0, half, NB):
+            to = pl.ds(pl.multiple_of(base + i, NB), NB)
+            slab[to, to] += jnp.where(eye, sm[1:2, i:i + NB], 0.0)
 
     nblk = FB // NB
 
@@ -161,8 +337,8 @@
             fac[b * NB:(b + 1) * NB, j * NB:(j + 1) * NB] = jnp.where(keep, piece, 0.0)
 
 
-def local(scale, pts, tgt, fw, fd, phw, phd, rdg, interpret=False):
-    rows, half = pts.shape[0], fd.shape[1]
+def local(scale, pts, fo, fp, fd, so, sp, sd):
+    rows, half = pts.shape[0] * 256, fd.shape[1]
     f32 = jnp.float32
     return pl.pallas_call(
         functools.partial(kernel, scale, "feat", "dp"),
@@ -177,31 +353,18 @@
             pltpu.VMEM((FB, FB), f32),
             pltpu.VMEM((NB, NB), f32),
             pltpu.VMEM((rows, half), jnp.bfloat16),
+            pltpu.VMEM((8, rows), jnp.bfloat16),
         ],
-        compiler_params=pltpu.CompilerParams(vmem_limit_bytes=60 * 1024 * 1024),
-        interpret=interpret,
-    )(pts, tgt, fw, fd, phw, phd, rdg)
+        compiler_params=pltpu.CompilerParams(vmem_limit_bytes=48 * 1024 * 1024),
+    )(pts, fo, fp, fd, so, sp, sd)
 
 
 def shards(points, freqs, phase, ridge, targets):
-    data_count = lax.axis_size("dp")
-    feat_count = lax.axis_size("feat")
-    feat = lax.axis_index("feat")
-    rows = points.shape[0]
-    half = freqs.shape[1]
-    scale = math.sqrt(2.0 / (rows * data_count))
-    pack = lax.all_gather(jnp.concatenate([points, targets], 0), "dp", axis=0)
-    points_all = pack[:, :rows].reshape(rows * data_count, -1)
-    targets_all = jnp.transpose(pack[:, rows:], (1, 0, 2)).reshape(targets.shape[0], -1)
-    small = jnp.stack([phase * TURN, ridge])
-    pair = [(i, i ^ 1) for i in range(feat_count)]
-    swap = [(d * feat_count + f, f * feat_count + d) for d in range(data_count) for f in range(feat_count)]
-    f_other, s_other = lax.ppermute(freqs, "feat", pair), lax.ppermute(small, "feat", pair)
-    f_tile, s_tile = lax.ppermute(freqs, ("dp", "feat"), swap), lax.ppermute(small, ("dp", "feat"), swap)
-    odd = lax.rem(feat, 2) == 1
-    fw = jnp.where(odd, jnp.concatenate([f_other, freqs], 1), jnp.concatenate([freqs, f_other], 1))
-    sw = jnp.where(odd, jnp.concatenate([s_other, small], 1), jnp.concatenate([small, s_other], 1))
-    return local(scale, points_all, targets_all, fw, f_tile, sw[0:1], s_tile[0:1], sw[1:2])
+    scale = math.sqrt(2.0 / (points.shape[0] * lax.axis_size("dp")))
+    pack = jnp.pad(jnp.concatenate([points, targets], 0), ((0, 8), (0, 0)))
+    small = jnp.stack([phase, ridge])
+    pts, other_f, other_s, tile_f, tile_s = gather(pack, freqs, small)
+    return local(scale, pts, freqs, other_f, tile_f, small, other_s, tile_s)
 
 
 def solution(mesh):

time: 155 us -> 112 us (0.72)
  waiting for transfers between devices: 46 us -> 0 us
  Pallas kernels: 73 us -> 101 us
  between operations: 14.1 us -> 0.65 us
  starting transfers between devices: 8.78 us -> 0 us
  other arithmetic: 5.71 us -> 2.89 us
    all_gather x1 -> x0, waiting for transfers between devices: 40.1 us -> none  [shards(): pack = lax.all_gather(jnp.concatenate([points, targets], 0), 'dp', axis=0)]
    pallas_call x0 -> x1, Pallas kernels: none -> 29.5 us  [gather(): pl.pallas_call(exchange, out_shape=(shape((2 * ZS,) + pack.shape, pack.dt...]
    ppermute x4 -> x0, starting transfers between devices: 8.75 us -> none  [the longest x1 4.61 us: shards(): lax.ppermute(small, ('dp', 'feat'), swap)]
    ppermute x4 -> x0, waiting for transfers between devices: 5.86 us -> none  [the longest x1 5.86 us: shards(): lax.ppermute(freqs, 'feat', pair)]
    unnamed x2 -> x14, local copies, waits for them, and re-layouts: 0.69 us -> 6.51 us
    slice x4 -> x0, local copies, waits for them, and re-layouts: 5.76 us -> none  [the longest x1 3.09 us: shards(): points_all = pack[:, :rows].reshape(rows * data_count, -1)]
    select_n x2 -> x0, other arithmetic: 2.75 us -> none  [the longest x1 1.98 us: shards(): jnp.where(odd, jnp.concatenate([f_other, freqs], 1), jnp.concatenate([fre...]
  transfers between devices with their start and end apart: 5 -> 0, of which waited for: 2 -> 0; matrix products, arithmetic and copies ran while one was open for 6% -> 0% of each run, Pallas kernels for 0% -> 0%
where the time goes in v2:
time: 112 us; the launch traced here: 111 us
  Pallas kernels  101 us (90%)
  local copies, waits for them, and re-layouts  6.51 us (6%)
  other arithmetic  2.89 us (3%)
    pallas_call x1, Pallas kernels, local(): pl.pallas_call(functools.partial(kernel, scale, 'feat', 'dp'), out_shape=...  71.6 us
    pallas_call x1, Pallas kernels, gather(): pl.pallas_call(exchange, out_shape=(shape((2 * ZS,) + pack.shape, pack.dt...  29.5 us
    unnamed x14, local copies, waits for them, and re-layouts  6.51 us

profile of v2, /device:TPU:1, one launch (start us, length us, event | category | flops | bytes accessed | tf_op | source)
XLA Modules:
  0.0 111.2 jit_solution(13502565117964339832)
XLA Ops:
  0.6 1.3 %pad_maximum_fusion.small.so = f32[2,512]{1,0:T(2,128)} fusion(f32[1,512]{1,0:T(1,128)} %bitcast.2, f32[1,512]{1,0:T(1,128)} %bitcast.3), kind=kLoop, calls=%fused_computation.4 | loop fusion | flops 1024 | bytes 8192 | tf_op jit(solution)/shard_map/stack | solution.py:365
  1.9 1.6 %fusion.2.pack = bf16[272,256]{1,0:T(8,128)(2,1)} fusion(bf16[8,256]{1,0:T(8,128)(2,1)} %param.9, bf16[256,256]{1,0:T(8,128)(2,1)} %param.5), kind=kLoop, calls=%fused_computation.3 | loop fusion | flops 487424 | bytes 274432 | tf_op jit(solution)/shard_map/concatenate | solution.py:364
  3.5 29.5 %shard_map.76 = (bf16[16,272,256]{2,1,0:T(8,128)(2,1)}, bf16[256,512]{1,0:T(8,128)(2,1)}, f32[2,512]{1,0:T(2,128)}, bf16[256,512]{1,0:T(8,128)(2,1)}, f32[2,512]{1,0:T(2,128)}) custom-call(bf16[272,256]{1,0:T(8,128)(2,1)} %fusion.2.pack, bf16[256,512]{1,0:T(8,128)(2,1)} %fo.1, f32[2,512]{1,0:T(2,128)} %pad_maximum_fusion.small.so), custom_call_target="tpu_custom_call" | custom-call | tf_op jit(solution)/shard_map/pallas_call | solution.py:171
  33.0 0.0 copy-start
  33.1 1.6 %copy-done = bf16[16,272,256]{2,1,0:T(8,128)(2,1)S(1)} copy-done((bf16[16,272,256]{2,1,0:T(8,128)(2,1)S(1)}, bf16[16,272,256]{2,1,0:T(8,128)(2,1)}, u32[]{:S(2)}) %copy-start) | copy-done | bytes 2228248
  34.7 0.0 copy-start.1
  34.7 0.9 copy-done.1
  35.6 0.0 copy-start.2
  35.6 0.9 copy-done.2
  36.6 0.0 copy-start.3
  36.6 0.9 copy-done.3
  37.5 0.0 copy-start.4
  37.5 0.7 copy-done.4
  38.2 0.0 copy-start.5
  38.2 0.7 copy-done.5
  38.9 0.0 copy-start.6
  38.9 0.7 copy-done.6
  39.6 71.6 %shard_map.77 = (f32[512,512]{1,0:T(8,128)}, f32[8,512]{1,0:T(8,128)}, f32[512,1024]{1,0:T(8,128)}) custom-call(bf16[16,272,256]{2,1,0:T(8,128)(2,1)S(1)} %copy-done, bf16[256,512]{1,0:T(8,128)(2,1)S(1)} %copy-done.1, bf16[256,512]{1,0:T(8,128)(2,1)S(1)} %copy-done.2, bf16[256,512]{1,0:T(8,128)(2,1)S(1)} %copy-done.3, f32[2,512]{1,0:T(2,128)S(1)} %copy-done.4, ...), custom_call_target="tpu_custom_call" | custom-call | tf_op jit(solution)/shard_map/pallas_call | solution.py:343
Async XLA Ops:
  33.0 1.6 %copy-start = (bf16[16,272,256]{2,1,0:T(8,128)(2,1)S(1)}, bf16[16,272,256]{2,1,0:T(8,128)(2,1)}, u32[]{:S(2)}) copy-start(bf16[16,272,256]{2,1,0:T(8,128)(2,1)} %get-tuple-element.8.pts) | copy-start | bytes 6684676
  34.7 0.9 copy-start.1
  35.6 0.9 copy-start.2
  36.6 0.9 copy-start.3
  37.5 0.7 copy-start.4
  38.2 0.7 copy-start.5
  38.9 0.7 copy-start.6

commit v3 on v1

v3 whole, which is shorter than its diff:
```python
import functools
import math

import jax
import jax.numpy as jnp
from jax import lax
from jax.experimental import pallas as pl
from jax.experimental.pallas import tpu as pltpu
from jax.sharding import PartitionSpec as P

FB = 1024
NB = 128
XS = 4
YS = 4
ZS = 8
HI = lax.Precision.HIGHEST
MESH = pl.DeviceIdType.MESH
TURN = 1.0 / (2.0 * math.pi)
C1, C3, C5, C7 = -6.283164044054801, 41.33714233314145, -81.34076747300007, 70.99341851060123


def cos_turns(turns, scale):
    r = turns - jnp.round(turns)
    u = jnp.abs(r) - 0.25
    w = u * u
    poly = ((C7 * scale * w + C5 * scale) * w + C3 * scale) * w + C1 * scale
    return poly * u


def tdot(left, right, precision=None):
    return lax.dot_general(
        left, right, (((0,), (0,)), ((), ())), precision=precision, preferred_element_type=jnp.float32
    )


def row_of(x, r):
    return jnp.broadcast_to(x[r:r + 1, :], x.shape)


def lane_of(x, c):
    return jnp.broadcast_to(x[:, c:c + 1], x.shape)


def leaf(blocks, one):
    n = NB // 8
    sub = lax.broadcasted_iota(jnp.int32, (8, NB), 0)
    lane = lax.broadcasted_iota(jnp.int32, (8, NB), 1)
    a = list(blocks)
    e = [jnp.where(lane == sub + 8 * m, 1.0, 0.0).astype(jnp.float32) for m in range(n)]

    def cols(m, k):
        return [lane_of(a[m], 8 * k + c) for c in range(8)]

    outs = []
    v, n1 = [x * one for x in cols(0, 0)], [x * one for x in cols(1, 0)]
    for k in range(n):
        pa, pe = a[k], e[k]
        has1, has2 = k + 1 < n, k + 2 < n
        far = {m: cols(m, k) for m in range(k + 2, n)}
        if has1:
            vn = cols(k + 1, k + 1)
        if has2:
            n2 = list(far[k + 2])
        rs = jnp.zeros((8, NB), jnp.float32)
        dv = jnp.zeros((8, NB), jnp.float32)
        for r in range(8):
            d = row_of(v[r], r)
            inv = 1.0 / d
            rs = jnp.where(sub == r, lax.rsqrt(d), rs)
            dv = jnp.where(sub == r, inv, dv)
            l = jnp.where(sub > r, v[r] * inv, 0.0)
            b = {c: row_of(v[c], r) for c in range(r + 1, 8)}
            ba, be = row_of(pa, r), row_of(pe, r)
            for c in b:
                v[c] = v[c] - l * b[c]
            pa = pa - l * ba
            pe = pe - l * be
            if has1:
                l1 = n1[r] * inv
                w = [row_of(n1[r], c) for c in range(8)]
                for c in b:
                    n1[c] = n1[c] - l1 * b[c]
                for c in range(8):
                    vn[c] = vn[c] - l1 * w[c]
                a[k + 1] = a[k + 1] - l1 * ba
                e[k + 1] = e[k + 1] - l1 * be
            if has2:
                l2 = n2[r] * inv
                for c in b:
                    n2[c] = n2[c] - l2 * b[c]
                a[k + 2] = a[k + 2] - l2 * ba
                e[k + 2] = e[k + 2] - l2 * be
        outs.append((pa * rs, pe * rs))
        if k + 3 < n:
            qa, qe = pa * dv, pe * dv
            for r in range(7, 0, -1):
                mult = jnp.where(sub < r, v[r] * dv, 0.0)
                qa = qa - mult * row_of(qa, r)
                qe = qe - mult * row_of(qe, r)
            ra = [row_of(qa, r) for r in range(8)]
            re = [row_of(qe, r) for r in range(8)]
            for m in range(k + 3, n):
                ma = [far[m][r] * ra[r] for r in range(8)]
                me = [far[m][r] * re[r] for r in range(8)]
                while len(ma) > 1:
                    ma = [ma[i] + ma[i + 1] for i in range(0, len(ma), 2)]
                    me = [me[i] + me[i + 1] for i in range(0, len(me), 2)]
                a[m] = a[m] - ma[0]
                e[m] = e[m] - me[0]
        if has1:
            v = vn
            if has2:
                n1 = [x * one for x in cols(k + 2, k + 1)]
    return outs


def fused(scale, pack, freqs, small, slab, gram, proj,
          points, other_f, other_s, tile_f, tile_s, wphi, cphi, tgt, slab_in, gram_out, gram_in, proj_in,
          up_send, up_recv, dn_send, dn_recv, pair_send, pair_recv, tree_recv, row_send, col_send,
          tile_send, tile_recv, swap_send, swap_recv, local_sem):
    data, feat = lax.axis_index("dp"), lax.axis_index("feat")
    z, core = data // 2, data % 2
    x, y = feat // YS, feat % YS
    block, half = 256, freqs.shape[1]
    odd = feat % 2
    own = pl.multiple_of(odd * half, half)
    oth = pl.multiple_of((1 - odd) * half, half)

    def at(zz, cc):
        return {"dp": zz * 2 + cc, "feat": feat}

    def near(xx, yy):
        return {"dp": data, "feat": xx * YS + yy}

    up, dn, mate = at((z + 1) % ZS, core), at((z + ZS - 1) % ZS, core), at(z, 1 - core)
    barrier = pltpu.get_barrier_semaphore()
    peers = [up, dn, mate]
    peers += [near((x + i) % XS, y) for i in range(1, XS)] + [near(x, (y + i) % YS) for i in range(1, YS)]
    for peer in peers:
        pl.semaphore_signal(barrier, inc=1, device_id=peer, device_id_type=MESH)
    pl.semaphore_wait(barrier, len(peers))

    first = 128
    pieces = (pl.ds(0, first), pl.ds(first, pack.shape[0] - first))
    sends = []

    def remote(src, dst, ssem, rsem, where):
        return pltpu.make_async_remote_copy(
            src_ref=src, dst_ref=dst, send_sem=ssem, recv_sem=rsem, device_id=where, device_id_type=MESH)

    def go(copy):
        copy.start()
        sends.append(copy)
        return copy

    def arrival(step, upward):
        return 7 if step == 4 else 2 * step - (1 if upward else 0)

    def ring(step, p, upward):
        src = pack if step == 0 else points.at[arrival(step, upward)]
        dst = points.at[arrival(step + 1, upward)]
        ssem, rsem, where = (up_send, up_recv, up) if upward else (dn_send, dn_recv, dn)
        return remote(src.at[pieces[p]], dst.at[pieces[p]], ssem.at[step, p], rsem.at[step, p], where)

    def ring_step(step):
        todo = [(0, True), (0, False), (1, True), (1, False)] if step < 4 else [(0, True), (1, False)]
        for p, upward in todo:
            ring(step - 1, p, upward).wait_recv()
            if step < 3 or (step == 3 and p == (0 if upward else 1)):
                go(ring(step, p, upward))

    for p in range(2):
        go(ring(0, p, True))
        go(ring(0, p, False))
    pair = near(x, y + 1 - 2 * (y % 2))
    pair_copies = [
        go(remote(small, other_s, pair_send.at[0], pair_recv.at[0], pair)),
        go(remote(freqs, other_f, pair_send.at[1], pair_recv.at[1], pair)),
    ]

    rx, ry = data // YS, data % YS
    parts = [(small, tile_s.at[0], None), (freqs, tile_f.at[0], pl.ds(0, 128)), (freqs, tile_f.at[0], pl.ds(128, 128))]

    def part(ref, cut):
        return ref if cut is None else ref.at[cut]

    def to_row(n, i):
        src, dst, cut = parts[n]
        return remote(part(src, cut), part(dst, cut), row_send.at[n, i], tree_recv.at[n], near((x + i + 1) % XS, y))

    def to_col(n, i, mine):
        src, dst, cut = parts[n]
        return remote(part(src if mine else dst, cut), part(dst, cut), col_send.at[n, i], tree_recv.at[n],
                      near(x, (y + i + 1) % YS))

    root = jnp.logical_and(x == rx, y == ry)
    mid = jnp.logical_and(x != rx, y == ry)

    @pl.when(root)
    def _():
        for n in range(3):
            for i in range(XS - 1):
                to_row(n, i).start()
            for i in range(YS - 1):
                to_col(n, i, True).start()
        a = pltpu.make_async_copy(freqs, tile_f.at[0], local_sem.at[0])
        b = pltpu.make_async_copy(small, tile_s.at[0], local_sem.at[1])
        a.start()
        b.start()
        a.wait()
        b.wait()

    def pass_on(n):
        @pl.when(mid)
        def _():
            to_row(n, 0).wait_recv()
            for i in range(YS - 1):
                to_col(n, i, False).start()

    def phi(i, src, sm, dst, base):
        block_ref = pack if i == 0 else points.at[i]

        def tile(j, _):
            cut = pl.ds(pl.multiple_of(j * 256, 256), 256)
            ang = jnp.dot(block_ref[0:block, :], src[:, cut], preferred_element_type=jnp.float32)
            to = pl.ds(pl.multiple_of(base + j * 256, 256), 256)
            dst[i * block:(i + 1) * block, to] = cos_turns(
                ang * TURN + sm[0:1, cut] * TURN, scale).astype(jnp.bfloat16)
            return 0

        lax.fori_loop(0, half // 256, tile, 0)

    def window(i):
        phi(i, freqs, small, wphi, own)
        phi(i, other_f, other_s, wphi, oth)
        block_ref = pack if i == 0 else points.at[i]
        tgt[:, i * block:(i + 1) * block] = block_ref[block:block + 8, :]

    def tiles(i):
        for j in range(2):
            phi(i, tile_f.at[j], tile_s.at[j], cphi, j * half)

    phi(0, freqs, small, wphi, own)
    tgt[:, 0:block] = pack[block:block + 8, :]
    ring_step(1)
    phi(1, freqs, small, wphi, own)
    pass_on(0)
    pass_on(1)
    pass_on(2)
    for copy in pair_copies:
        copy.wait_recv()
    phi(0, other_f, other_s, wphi, oth)
    phi(1, other_f, other_s, wphi, oth)
    tgt[:, block:2 * block] = points[1, block:block + 8, :]
    ring_step(2)
    for i in (2, 3):
        window(i)

    @pl.when(y != ry)
    def _():
        for n in range(3):
            to_col(n, 0, False).wait_recv()

    tile_copies = [
        go(remote(tile_s.at[0], tile_s.at[1], tile_send.at[0], tile_recv.at[0], mate)),
        go(remote(tile_f.at[0], tile_f.at[1], tile_send.at[1], tile_recv.at[1], mate)),
    ]
    window(4)
    ring_step(3)
    k0 = 4 * block
    for i in range(0, FB, 256):
        slab[i:i + 256, i:] = tdot(wphi[0:k0, i:i + 256], wphi[0:k0, i:])
    for i in (5, 6):
        window(i)
    for copy in tile_copies:
        copy.wait_recv()
    for i in range(0, 3):
        tiles(i)
    ring_step(4)
    window(7)

    def swap(n):
        cut = (pl.ds(n * 256, 256), pl.ds(n * 256, FB - n * 256))
        return remote(slab.at[cut], slab_in.at[cut], swap_send.at[n], swap_recv.at[n], mate)

    for n in range(4):
        i = n * 256
        slab[i:i + 256, i:] += tdot(wphi[k0:, i:i + 256], wphi[k0:, i:])
        if n > 0:
            swap(n - 1).start()
    tiles(3)
    swap(3).start()
    for i in range(4, 8):
        tiles(i)
    own_cut = pl.ds(own, half)
    gram_out[...] = tdot(wphi[:, own_cut], cphi[:, half:])
    proj[...] = jnp.dot(tgt[...], wphi[:, own_cut], preferred_element_type=jnp.float32)
    gram[...] = tdot(wphi[:, own_cut], cphi[:, 0:half])
    gram_copy = go(remote(gram_out, gram_in, swap_send.at[4], swap_recv.at[4], mate))
    proj_copy = remote(proj, proj_in, swap_send.at[5], swap_recv.at[5], mate)
    proj_copy.start()

    eye = lax.broadcasted_iota(jnp.int32, (NB, NB), 0) == lax.broadcasted_iota(jnp.int32, (NB, NB), 1)
    for n in range(4):
        swap(n).wait_send()
        swap(n).wait_recv()
        i = n * 256
        slab[i:i + 256, i:] += slab_in[i:i + 256, i:]
    for sm, base in ((small, own), (other_s, oth)):
        for i in range(0, half, NB):
            to = pl.ds(pl.multiple_of(base + i, NB), NB)
            slab[to, to] += jnp.where(eye, sm[1:2, i:i + NB], 0.0)
    gram_copy.wait_recv()
    gram[...] += gram_in[...]

    @pl.when(feat == data)
    def _():
        for i in range(0, half, NB):
            gram[i:i + NB, i:i + NB] += jnp.where(eye, small[1:2, i:i + NB], 0.0)

    proj_copy.wait_recv()
    proj_copy.wait_send()
    proj[...] += proj_in[...]

    @pl.when(root)
    def _():
        for n in range(3):
            for i in range(XS - 1):
                to_row(n, i).wait_send()

    @pl.when(y == ry)
    def _():
        for n in range(3):
            for i in range(YS - 1):
                to_col(n, i, False).wait_send()

    for copy in sends:
        copy.wait_send()


def assemble(scale, pack, freqs, small):
    dma = pltpu.SemaphoreType.DMA
    vmem = pl.BlockSpec(memory_space=pltpu.VMEM)
    f32, bf16 = jnp.float32, jnp.bfloat16
    half = freqs.shape[1]
    shape = jax.ShapeDtypeStruct
    rows = ZS * 256
    return pl.pallas_call(
        functools.partial(fused, scale),
        out_shape=(shape((FB, FB), f32), shape((half, half), f32), shape((8, half), f32)),
        in_specs=[vmem] * 3,
        out_specs=(vmem,) * 3,
        scratch_shapes=[
            pltpu.VMEM((ZS,) + pack.shape, bf16),
            pltpu.VMEM(freqs.shape, bf16), pltpu.VMEM(small.shape, f32),
            pltpu.VMEM((2,) + freqs.shape, bf16), pltpu.VMEM((2,) + small.shape, f32),
            pltpu.VMEM((rows, FB), bf16), pltpu.VMEM((rows, 2 * half), bf16), pltpu.VMEM((8, rows), bf16),
            pltpu.VMEM((FB, FB), f32), pltpu.VMEM((half, half), f32), pltpu.VMEM((half, half), f32),
            pltpu.VMEM((8, half), f32),
            dma((4, 2)), dma((4, 2)), dma((4, 2)), dma((4, 2)),
            dma((2,)), dma((2,)), dma((3,)), dma((3, 3)), dma((3, 3)),
            dma((2,)), dma((2,)), dma((6,)), dma((6,)), dma((2,)),
        ],
        compiler_params=pltpu.CompilerParams(
            collective_id=0, has_side_effects=True, vmem_limit_bytes=50 * 1024 * 1024),
    )(pack, freqs, small)


def chol(feat_axis, src, fac, slab, ue, ones, sem):
    half = fac.shape[0]
    odd = lax.rem(lax.axis_index(feat_axis), FB // half)
    own = pl.multiple_of(odd * half, half)
    loads = [
        pltpu.make_async_copy(src.at[pl.ds(i * NB, NB), pl.ds(i * NB, FB - i * NB)],
                              slab.at[pl.ds(i * NB, NB), pl.ds(i * NB, FB - i * NB)], sem.at[i])
        for i in range(FB // NB)
    ]
    for load in loads:
        load.start()
    for load in loads:
        load.wait()

    nblk = FB // NB
    ones[...] = jnp.ones_like(ones)

    def step(k, _):
        at = pl.multiple_of(k * NB, NB)
        blocks = [slab[pl.ds(pl.multiple_of(at + 8 * m, 8), 8), pl.ds(at, NB)] for m in range(NB // 8)]
        sub = lax.broadcasted_iota(jnp.int32, (8, NB), 0)
        lane = lax.broadcasted_iota(jnp.int32, (8, NB), 1)
        for m, (u, x) in enumerate(leaf(blocks, ones[...])):
            slab[pl.ds(pl.multiple_of(at + 8 * m, 8), 8), pl.ds(at, NB)] = jnp.where(lane >= sub + 8 * m, u, 0.0)
            ue[8 * m:8 * m + 8, :] = x
        for kk in range(nblk - 1):
            @pl.when(k == kk)
            def _():
                lo, mid = kk * NB, (kk + 1) * NB
                u12 = jnp.dot(ue[...], slab[lo:mid, mid:], precision=HI, preferred_element_type=jnp.float32)
                slab[lo:mid, mid:] = u12
                for i in range(mid, FB, 256):
                    w = min(256, FB - i)
                    slab[i:i + w, i:] -= tdot(u12[:, i - mid:i - mid + w], u12[:, i - mid:], HI)
        return 0

    lax.fori_loop(0, nblk, step, 0)

    for b in range(half // NB):
        for j in range(nblk):
            piece = jnp.transpose(slab[j * NB:(j + 1) * NB, pl.ds(pl.multiple_of(own + b * NB, NB), NB)])
            keep = j * NB <= own + b * NB
            fac[b * NB:(b + 1) * NB, j * NB:(j + 1) * NB] = jnp.where(keep, piece, 0.0)


def factor(slab):
    f32 = jnp.float32
    return pl.pallas_call(
        functools.partial(chol, "feat"),
        out_shape=jax.ShapeDtypeStruct((FB // 2, FB), f32),
        in_specs=[pl.BlockSpec(memory_space=pl.ANY)],
        out_specs=pl.BlockSpec(memory_space=pltpu.VMEM),
        scratch_shapes=[
            pltpu.VMEM((FB, FB), f32),
            pltpu.VMEM((NB, NB), f32),
            pltpu.VMEM((8, NB), f32),
            pltpu.SemaphoreType.DMA((FB // NB,)),
        ],
        compiler_params=pltpu.CompilerParams(vmem_limit_bytes=48 * 1024 * 1024),
    )(slab)


def shards(points, freqs, phase, ridge, targets):
    scale = math.sqrt(2.0 / (points.shape[0] * lax.axis_size("dp")))
    pack = jnp.pad(jnp.concatenate([points, targets], 0), ((0, 8), (0, 0)))
    slab, gram, proj = assemble(scale, pack, freqs, jnp.stack([phase, ridge]))
    return gram, proj, factor(slab)


def solution(mesh):
    in_specs = (P("dp", None), P(None, "feat"), P("feat"), P("feat"), P(None, "dp"))
    out_specs = (P("feat", "dp"), P(None, "feat"), P("feat", None))
    return jax.shard_map(shards, mesh=mesh, in_specs=in_specs, out_specs=out_specs, check_vma=False)
```

time: 155 us -> 87.3 us (0.56)
  waiting for transfers between devices: 46 us -> 0 us
  between operations: 14.1 us -> 0.67 us
  starting transfers between devices: 8.78 us -> 0 us
  Pallas kernels: 73 us -> 79.7 us
  other arithmetic: 5.71 us -> 1.64 us
  local copies, waits for them, and re-layouts: 6.46 us -> 4.7 us
    all_gather x1 -> x0, waiting for transfers between devices: 40.1 us -> none  [shards(): pack = lax.all_gather(jnp.concatenate([points, targets], 0), 'dp', axis=0)]
    ppermute x4 -> x0, starting transfers between devices: 8.75 us -> none  [the longest x1 4.61 us: shards(): lax.ppermute(small, ('dp', 'feat'), swap)]
    pallas_call x1 -> x2, Pallas kernels: 73 us -> 79.7 us  [the longest x1 46.9 us: assemble(): pl.pallas_call(functools.partial(fused, scale), out_shape=(shape((FB, FB)...]
    ppermute x4 -> x0, waiting for transfers between devices: 5.86 us -> none  [the longest x1 5.86 us: shards(): lax.ppermute(freqs, 'feat', pair)]
    slice x4 -> x0, local copies, waits for them, and re-layouts: 5.76 us -> none  [the longest x1 3.09 us: shards(): points_all = pack[:, :rows].reshape(rows * data_count, -1)]
    unnamed x2 -> x6, local copies, waits for them, and re-layouts: 0.69 us -> 4.7 us
    select_n x2 -> x0, other arithmetic: 2.75 us -> none  [the longest x1 1.98 us: shards(): jnp.where(odd, jnp.concatenate([f_other, freqs], 1), jnp.concatenate([fre...]
  transfers between devices with their start and end apart: 5 -> 0, of which waited for: 2 -> 0; matrix products, arithmetic and copies ran while one was open for 6% -> 0% of each run, Pallas kernels for 0% -> 0%
where the time goes in v3:
time: 87.3 us; the launch traced here: 86.7 us
  Pallas kernels  79.7 us (91%)
  local copies, waits for them, and re-layouts  4.7 us (5%)
  other arithmetic  1.64 us (2%)
    pallas_call x1, Pallas kernels, assemble(): pl.pallas_call(functools.partial(fused, scale), out_shape=(shape((FB, FB)...  46.9 us
    pallas_call x1, Pallas kernels, factor(): pl.pallas_call(functools.partial(chol, 'feat'), out_shape=jax.ShapeDtypeS...  32.8 us
    unnamed x6, local copies, waits for them, and re-layouts  4.7 us

profile of v3, /device:TPU:1, one launch (start us, length us, event | category | flops | bytes accessed | tf_op | source)
XLA Modules:
  0.0 86.7 jit_solution(7183950995169079562)
XLA Ops:
  0.6 0.7 pad_maximum_fusion.small
  1.3 0.9 %fusion.2.pack = bf16[272,256]{1,0:T(8,128)(2,1)S(1)} fusion(bf16[8,256]{1,0:T(8,128)(2,1)} %param.9, bf16[256,256]{1,0:T(8,128)(2,1)} %param.5), kind=kLoop, calls=%fused_computation.3 | loop fusion | flops 487424 | bytes 274432 | tf_op jit(solution)/shard_map/concatenate | solution.py:433
  2.3 0.0 copy-start.1
  2.3 0.9 %copy-done.1 = bf16[256,512]{1,0:T(8,128)(2,1)S(1)} copy-done((bf16[256,512]{1,0:T(8,128)(2,1)S(1)}, bf16[256,512]{1,0:T(8,128)(2,1)}, u32[]{:S(2)}) %copy-start.1) | copy-done | bytes 262168
  3.2 46.9 %shard_map.76 = (f32[1024,1024]{1,0:T(8,128)}, f32[512,512]{1,0:T(8,128)S(1)}, f32[8,512]{1,0:T(8,128)S(1)}) custom-call(bf16[272,256]{1,0:T(8,128)(2,1)S(1)} %fusion.2.pack, bf16[256,512]{1,0:T(8,128)(2,1)S(1)} %copy-done.1, f32[2,512]{1,0:T(2,128)S(1)} %pad_maximum_fusion.small), custom_call_target="tpu_custom_call" | custom-call | tf_op jit(solution)/shard_map/pallas_call | solution.py:348
  50.1 0.0 copy-start
  50.1 2.2 %copy-done = f32[1024,1024]{1,0:T(8,128)S(1)} copy-done((f32[1024,1024]{1,0:T(8,128)S(1)}, f32[1024,1024]{1,0:T(8,128)}, u32[]{:S(2)}) %copy-start) | copy-done | bytes 4194328
  52.3 32.8 %shard_map.77 = f32[512,1024]{1,0:T(8,128)} custom-call(f32[1024,1024]{1,0:T(8,128)S(1)} %copy-done), custom_call_target="tpu_custom_call" | custom-call | tf_op jit(solution)/shard_map/pallas_call | solution.py:416
  85.1 1.0 %copy.10 = f32[512,512]{1,0:T(8,128)} copy(f32[512,512]{1,0:T(8,128)S(1)} %get-tuple-element.12) | data formatting | bytes 2097152
  86.1 0.6 copy.11
Async XLA Ops:
  2.3 1.0 %copy-start.1 = (bf16[256,512]{1,0:T(8,128)(2,1)S(1)}, bf16[256,512]{1,0:T(8,128)(2,1)}, u32[]{:S(2)}) copy-start(bf16[256,512]{1,0:T(8,128)(2,1)} %freqs.1) | copy-start | bytes 786436
  50.1 2.2 %copy-start = (f32[1024,1024]{1,0:T(8,128)S(1)}, f32[1024,1024]{1,0:T(8,128)}, u32[]{:S(2)}) copy-start(f32[1024,1024]{1,0:T(8,128)} %get-tuple-element.8.src) | copy-start | bytes 12582916
